TPU v7x, 32 devices: a whole 2x2x4 slice. The times are simulated.
32 devices in a mesh: cp: 8 (over y, x, core), tp: 4 (over z).
Axes of the slice: x: 2, y: 2, z: 4, core: 2. Of those that a mesh axis runs over, the one named last changes fastest.
Arguments:
- queries: bfloat16 [6144, 5120], P('cp', 'tp'), may hold values from -36 to 36
- keys: bfloat16 [6144, 1024], P('cp', 'tp'), may hold values from -5 to 5
- values: bfloat16 [6144, 1024], P('cp', 'tp'), may hold values from -6 to 6
- doc_lengths: int32 [8], replicated, may hold values from 1 to 1536, 6144 in all
Outputs:
- attended: bfloat16 [6144, 5120], P(('cp', 'tp'))
Inputs may be any that keep to these rules, and one draw needn't show every extreme that they name: `doc_lengths`: they sum to 6144, and one of them is exactly 1536.
All inputs are finite; a program needn't handle non-finite values.
Results may differ from a plain program's by a relative error of at most 0.0038.
Values may be sent and summed in bfloat16 or wider, within the bound.
A program may use at most 256 MiB of HBM per device.

v0:
```python
import jax
import jax.numpy as jnp
from jax import lax
from jax.sharding import PartitionSpec as P

HEAD = 128
DOC_DEVS = 2
negative = -1e30


def doc_index(positions, doc_ends):
    return jnp.sum((positions[..., None] >= doc_ends).astype(jnp.int32), axis=-1)


def on_device(queries, keys, values, doc_lengths):
    tok_rows, q_cols = queries.shape
    kv_cols = keys.shape[1]
    kv_local = kv_cols // HEAD
    group_size = q_cols // kv_cols
    half_rows = tok_rows // 2
    cp_size = lax.axis_size("cp")
    my_index = lax.axis_index("cp")
    stretch_span = 2 * min(DOC_DEVS, cp_size // 2)
    doc_ends = jnp.cumsum(doc_lengths)
    paired = jnp.stack([keys, values])
    kv_bank = lax.all_gather(paired[None], "cp", axis=0, tiled=True)
    bank_slots = kv_bank.shape[0]
    kv_bank = kv_bank.reshape(bank_slots, 2, 2, half_rows, kv_local, HEAD)
    stretch_ids = jnp.stack([my_index, 2 * cp_size - 1 - my_index])
    offsets = jnp.arange(half_rows, dtype=jnp.int32)
    q_pos = stretch_ids[:, None] * half_rows + offsets[None, :]
    q_doc = doc_index(q_pos, doc_ends)
    q_blocks = queries.reshape(2, half_rows, kv_local, group_size, HEAD)
    scale = float(HEAD) ** (-0.5)

    def fetch_block(kv_slot, kv_part):
        kv_piece = lax.dynamic_index_in_dim(kv_bank, kv_slot, 0, keepdims=False)
        return lax.dynamic_index_in_dim(kv_piece, kv_part, 1, keepdims=False)

    def one_tile(tile_step, state_now):
        needed = stretch_ids - tile_step
        present = needed >= 0
        clamped = jnp.maximum(needed, 0)
        device_ids = jnp.where(clamped < cp_size, clamped, 2 * cp_size - 1 - clamped)
        kv_part = (clamped >= cp_size).astype(jnp.int32)
        kv_slot = jnp.clip(device_ids, 0, bank_slots - 1)
        k_pos = clamped[:, None] * half_rows + offsets[None, :]
        k_doc = doc_index(k_pos, doc_ends)
        allowed = (
            present[:, None, None]
            & (k_doc[:, None, :] == q_doc[:, :, None])
            & (k_pos[:, None, :] <= q_pos[:, :, None])
        )
        running_max, running_sum, running_out = state_now
        pieces = jnp.stack([fetch_block(kv_slot[which], kv_part[which]) for which in range(2)])
        scores = (
            jnp.einsum(
                "cqhjd,ckhd->cqhjk", q_blocks, pieces[:, 0], preferred_element_type=jnp.float32
            )
            * scale
        )
        allowed_wide = allowed[:, :, None, None, :]
        scores = jnp.where(allowed_wide, scores, negative)
        new_max = jnp.maximum(running_max, jnp.max(scores, axis=-1))
        weights = jnp.where(allowed_wide, jnp.exp(scores - new_max[..., None]), 0.0)
        rescale = jnp.exp(running_max - new_max)
        new_sum = rescale * running_sum + jnp.sum(weights, axis=-1)
        product = jnp.einsum(
            "cqhjk,ckhd->cqhjd",
            weights.astype(jnp.bfloat16),
            pieces[:, 1],
            preferred_element_type=jnp.float32,
        )
        new_out = rescale[..., None] * running_out + product
        return (new_max, new_sum, new_out)

    start_state = (
        jnp.full((2, half_rows, kv_local, group_size), negative, jnp.float32),
        jnp.zeros((2, half_rows, kv_local, group_size), jnp.float32),
        jnp.zeros((2, half_rows, kv_local, group_size, HEAD), jnp.float32),
    )
    final_max, final_sum, final_out = lax.fori_loop(0, stretch_span + 1, one_tile, start_state)
    attended = (final_out / final_sum[..., None]).reshape(tok_rows, q_cols).astype(jnp.bfloat16)
    return lax.all_to_all(attended, "tp", split_axis=0, concat_axis=1, tiled=True)


def solution(mesh):
    in_specs = (P("cp", "tp"), P("cp", "tp"), P("cp", "tp"), P())
    out_specs = P(("cp", "tp"), None)
    return jax.shard_map(
        on_device, mesh=mesh, in_specs=in_specs, out_specs=out_specs, check_vma=False
    )
```

profile of v0, /device:TPU:0, one launch (start us, length us, event | category | flops | bytes accessed | tf_op | source)
XLA Modules:
  0.0 252.6 jit_solution(6885560735671889990)
XLA Ops:
  6.5 2.1 pad_maximum_fusion.1
  9.5 5.7 %reshape.167 = bf16[2,384,2,5,128]{4,3,2,1,0:T(8,128)(2,1)} reshape(bf16[768,1280]{1,0:T(8,128)(2,1)} %param.6) | data formatting | bytes 3932160 | tf_op jit(solution)/shard_map/reshape | solution.py:33
  15.2 2.4 copy.32
  17.9 39.5 %all-gather.3.cloned.1.call-done = bf16[16,768,256]{2,1,0:T(8,128)(2,1)} async-done(((bf16[2,768,256]{2,1,0:T(8,128)(2,1)}), bf16[16,768,256]{2,1,0:T(8,128)(2,1)}) %all-gather.3.cloned.1.call-update) | async-done | bytes 6291472 | tf_op jit(solution)/shard_map/all_gather | solution.py:26
  57.4 9.8 %reshape.161 = bf16[8,2,2,384,2,128]{5,4,3,2,1,0:T(2,128)(2,1)} reshape(bf16[16,768,256]{2,1,0:T(8,128)(2,1)} %all-gather.3.cloned.1.call-done) | data formatting | bytes 12582912 | tf_op jit(solution)/shard_map/reshape | solution.py:28
  67.1 7.1 %copy.31 = bf16[8,2,2,384,2,128]{5,3,4,1,2,0:T(8,128)(2,1)} copy(bf16[8,2,2,384,2,128]{5,4,3,2,1,0:T(2,128)(2,1)} %reshape.161) | data formatting | bytes 12582912
  74.2 108.8 %while.21 = (s32[]{:T(128)}, f32[2,384,2,5]{1,3,2,0:T(8,128)S(1)}, f32[2,384,2,5]{1,3,2,0:T(8,128)S(1)}, f32[2,384,2,5,128]{1,4,3,2,0:T(8,128)}, s32[2]{0:T(128)...) while((s32[]{:T(128)}, f32[2,384,2,5]{1,3,2,0:T(8,128)S(1)}, ...), condition=%wide.region_6.7_spmd.clone, body=%wide.region_2.6_spmd.clone.sunk | while | flops 1554047232 | bytes 50061820 | solution.py:82
  83.3 1.2 dynamic-slice_bitcast_fusion.3
  84.5 2.0 fusion.42
  86.5 2.9 %fusion.43 = f32[2,384,2,5]{1,3,2,0:T(8,128)S(1)} fusion(f32[2,2,384,384,5]{3,2,4,1,0:T(8,128)S(1)} %get-tuple-element.508, f32[2,384,2,5]{1,3,2,0:T(8,128)S(1)} %select_maximum_fusion.2, pred[2,384,384]{1,2,0:T(8,128)(4,1)S(1)} %compare_and_fusion.2), kind=kLoop, calls=%fused_computation.6.clone.1 | loop fusion | flops 14737920 | bytes 12152832 | tf_op jit(solution)/shard_map/while/body/eval_jaxpr/reduce_sum | solution.py:67
  89.4 5.3 %bitcast_add_fusion.2 = f32[2,384,2,5,128]{1,4,3,2,0:T(8,128)} fusion(f32[2,384,2,5,128]{1,4,3,2,0:T(8,128)} %get-tuple-element.529, f32[2,2,384,384,5]{3,2,4,1,0:T(8,128)S(1)} %get-tuple-element.508, f32[2,384,2,5]{1,3,2,0:T(8,128)S(1)} %select_maximum_fusion.2, pred[2,384,384]{1,2,0:T(8,128)(4,1)S(1)} %compare_and_fusion.2, ...), kind=kOutput, calls=%fused_computation.9.clone.1 | convolution fusion | flops 773455872 | bytes 20803584 | tf_op jit(solution)/shard_map/while/body/eval_jaxpr/cqhjk,ckhd->cqhjd/dot_general | solution.py:68
  103.8 1.2 dynamic-slice_bitcast_fusion.3
  105.0 2.0 fusion.42
  107.1 2.9 %fusion.43 = f32[2,384,2,5]{1,3,2,0:T(8,128)S(1)} fusion(f32[2,2,384,384,5]{3,2,4,1,0:T(8,128)S(1)} %get-tuple-element.508, f32[2,384,2,5]{1,3,2,0:T(8,128)S(1)} %select_maximum_fusion.2, pred[2,384,384]{1,2,0:T(8,128)(4,1)S(1)} %compare_and_fusion.2), kind=kLoop, calls=%fused_computation.6.clone.1 | loop fusion | flops 14737920 | bytes 12152832 | tf_op jit(solution)/shard_map/while/body/eval_jaxpr/reduce_sum | solution.py:67
  110.0 6.8 %bitcast_add_fusion.2 = f32[2,384,2,5,128]{1,4,3,2,0:T(8,128)} fusion(f32[2,384,2,5,128]{1,4,3,2,0:T(8,128)} %get-tuple-element.529, f32[2,2,384,384,5]{3,2,4,1,0:T(8,128)S(1)} %get-tuple-element.508, f32[2,384,2,5]{1,3,2,0:T(8,128)S(1)} %select_maximum_fusion.2, pred[2,384,384]{1,2,0:T(8,128)(4,1)S(1)} %compare_and_fusion.2, ...), kind=kOutput, calls=%fused_computation.9.clone.1 | convolution fusion | flops 773455872 | bytes 20803584 | tf_op jit(solution)/shard_map/while/body/eval_jaxpr/cqhjk,ckhd->cqhjd/dot_general | solution.py:68
  125.9 1.2 dynamic-slice_bitcast_fusion.3
  127.1 2.0 fusion.42
  129.1 2.9 %fusion.43 = f32[2,384,2,5]{1,3,2,0:T(8,128)S(1)} fusion(f32[2,2,384,384,5]{3,2,4,1,0:T(8,128)S(1)} %get-tuple-element.508, f32[2,384,2,5]{1,3,2,0:T(8,128)S(1)} %select_maximum_fusion.2, pred[2,384,384]{1,2,0:T(8,128)(4,1)S(1)} %compare_and_fusion.2), kind=kLoop, calls=%fused_computation.6.clone.1 | loop fusion | flops 14737920 | bytes 12152832 | tf_op jit(solution)/shard_map/while/body/eval_jaxpr/reduce_sum | solution.py:67
  132.1 6.8 %bitcast_add_fusion.2 = f32[2,384,2,5,128]{1,4,3,2,0:T(8,128)} fusion(f32[2,384,2,5,128]{1,4,3,2,0:T(8,128)} %get-tuple-element.529, f32[2,2,384,384,5]{3,2,4,1,0:T(8,128)S(1)} %get-tuple-element.508, f32[2,384,2,5]{1,3,2,0:T(8,128)S(1)} %select_maximum_fusion.2, pred[2,384,384]{1,2,0:T(8,128)(4,1)S(1)} %compare_and_fusion.2, ...), kind=kOutput, calls=%fused_computation.9.clone.1 | convolution fusion | flops 773455872 | bytes 20803584 | tf_op jit(solution)/shard_map/while/body/eval_jaxpr/cqhjk,ckhd->cqhjd/dot_general | solution.py:68
  148.0 1.2 dynamic-slice_bitcast_fusion.3
  149.1 2.0 fusion.42
  151.2 2.9 %fusion.43 = f32[2,384,2,5]{1,3,2,0:T(8,128)S(1)} fusion(f32[2,2,384,384,5]{3,2,4,1,0:T(8,128)S(1)} %get-tuple-element.508, f32[2,384,2,5]{1,3,2,0:T(8,128)S(1)} %select_maximum_fusion.2, pred[2,384,384]{1,2,0:T(8,128)(4,1)S(1)} %compare_and_fusion.2), kind=kLoop, calls=%fused_computation.6.clone.1 | loop fusion | flops 14737920 | bytes 12152832 | tf_op jit(solution)/shard_map/while/body/eval_jaxpr/reduce_sum | solution.py:67
  154.1 6.8 %bitcast_add_fusion.2 = f32[2,384,2,5,128]{1,4,3,2,0:T(8,128)} fusion(f32[2,384,2,5,128]{1,4,3,2,0:T(8,128)} %get-tuple-element.529, f32[2,2,384,384,5]{3,2,4,1,0:T(8,128)S(1)} %get-tuple-element.508, f32[2,384,2,5]{1,3,2,0:T(8,128)S(1)} %select_maximum_fusion.2, pred[2,384,384]{1,2,0:T(8,128)(4,1)S(1)} %compare_and_fusion.2, ...), kind=kOutput, calls=%fused_computation.9.clone.1 | convolution fusion | flops 773455872 | bytes 20803584 | tf_op jit(solution)/shard_map/while/body/eval_jaxpr/cqhjk,ckhd->cqhjd/dot_general | solution.py:68
  170.0 1.2 dynamic-slice_bitcast_fusion.3
  171.2 2.0 fusion.42
  173.3 2.9 %fusion.43 = f32[2,384,2,5]{1,3,2,0:T(8,128)S(1)} fusion(f32[2,2,384,384,5]{3,2,4,1,0:T(8,128)S(1)} %get-tuple-element.508, f32[2,384,2,5]{1,3,2,0:T(8,128)S(1)} %select_maximum_fusion.2, pred[2,384,384]{1,2,0:T(8,128)(4,1)S(1)} %compare_and_fusion.2), kind=kLoop, calls=%fused_computation.6.clone.1 | loop fusion | flops 14737920 | bytes 12152832 | tf_op jit(solution)/shard_map/while/body/eval_jaxpr/reduce_sum | solution.py:67
  176.2 6.8 %bitcast_add_fusion.2 = f32[2,384,2,5,128]{1,4,3,2,0:T(8,128)} fusion(f32[2,384,2,5,128]{1,4,3,2,0:T(8,128)} %get-tuple-element.529, f32[2,2,384,384,5]{3,2,4,1,0:T(8,128)S(1)} %get-tuple-element.508, f32[2,384,2,5]{1,3,2,0:T(8,128)S(1)} %select_maximum_fusion.2, pred[2,384,384]{1,2,0:T(8,128)(4,1)S(1)} %compare_and_fusion.2, ...), kind=kOutput, calls=%fused_computation.9.clone.1 | convolution fusion | flops 773455872 | bytes 20803584 | tf_op jit(solution)/shard_map/while/body/eval_jaxpr/cqhjk,ckhd->cqhjd/dot_general | solution.py:68
  183.0 3.8 %divide_convert_fusion = bf16[2,384,2,5,128]{1,4,3,2,0:T(8,128)(2,1)} fusion(f32[2,384,2,5,128]{1,4,3,2,0:T(8,128)} %get-tuple-element.300, f32[2,384,2,5]{1,3,2,0:T(8,128)S(1)} %get-tuple-element.301), kind=kLoop, calls=%fused_computation.40 | loop fusion | flops 1966080 | bytes 5928960 | tf_op jit(solution)/shard_map/convert_element_type | solution.py:83
  186.8 3.8 %copy.41 = bf16[2,384,2,5,128]{4,3,2,1,0:T(8,128)(2,1)S(1)} copy(bf16[2,384,2,5,128]{1,4,3,2,0:T(8,128)(2,1)} %divide_convert_fusion) | data formatting | bytes 3932160 | tf_op jit(solution)/shard_map/convert_element_type | solution.py:83
  190.7 3.2 %reshape.168 = bf16[4,192,1280]{2,1,0:T(8,128)(2,1)} reshape(bf16[2,384,2,5,128]{4,3,2,1,0:T(8,128)(2,1)S(1)} %copy.41) | data formatting | bytes 3932160 | tf_op jit(solution)/shard_map/convert_element_type | solution.py:83
  193.9 50.4 %all_to_all.16 = bf16[4,192,1280]{2,1,0:T(8,128)(2,1)S(1)} all-to-all(bf16[4,192,1280]{2,1,0:T(8,128)(2,1)} %reshape.168), channel_id=1, replica_groups=mesh['cp'=8,'tp'=4] {'tp'}, dimensions={0} | all-to-all | bytes 3932160 | tf_op jit(solution)/shard_map/all_to_all | solution.py:84
  244.3 1.5 copy.45
  (59 shorter events, 10.0 us)
Async XLA Ops:
  6.5 50.8 %all-gather.3.cloned.1.call-start = ((), (), s32[]{:S(2)}) async-start(), calls=%async_computation.1 | async-start | bytes 7077888 | tf_op jit(solution)/shard_map/all_gather | solution.py:26
Sparse Core Ops, SparseCore 0:
  9.2 48.1 all-gather.2
where the time goes:
time: 254 us; the launch traced here: 253 us
  blocking collectives  50.4 us (20%)
  local copies, waits for them, and re-layouts  45.3 us (18%)
  matrix products  42.8 us (17%)
  waiting for transfers between devices  39.5 us (16%)
  loops' own time  36.9 us (15%)
  other arithmetic  24.3 us (10%)
  between operations  13.4 us (5%)
    all_to_all x1, blocking collectives, on_device(): lax.all_to_all(attended, 'tp', split_axis=0, concat_axis=1, tiled=True)  50.4 us
    all_gather x1, waiting for transfers between devices, on_device(): kv_bank = lax.all_gather(paired[None], 'cp', axis=0, tiled=True)  39.5 us
    another operation x1, loops' own time, on_device(): lax.fori_loop(0, stretch_span + 1, one_tile, start_state)  36.9 us
    dot_general x5, matrix products, one_tile(): jnp.einsum('cqhjk,ckhd->cqhjd', weights.astype(jnp.bfloat16), pieces[:, 1...  32.5 us
    reduce_sum x5, other arithmetic, one_tile(): new_sum = rescale * running_sum + jnp.sum(weights, axis=-1)  14.3 us
    dot_general x5, matrix products, one_tile(): jnp.einsum('cqhjd,ckhd->cqhjk', q_blocks, pieces[:, 0], preferred_element...  10.2 us
    reshape x1, local copies, waits for them, and re-layouts, on_device(): kv_bank = kv_bank.reshape(bank_slots, 2, 2, half_rows, kv_local, HEAD)  9.75 us
    unnamed x2, local copies, waits for them, and re-layouts  9.53 us
  transfers between devices with their start and end apart: 1, of which 1 were waited for; matrix products, arithmetic and copies ran while one was open for 4% of the time, Pallas kernels for 0%

commit v1 on v0

--- a/solution.py
+++ b/solution.py
@@ -6,6 +6,12 @@
 HEAD = 128
 DOC_DEVS = 2
 negative = -1e30
+
+
+def stacked_exchange(shard, name, split, join):
+    pieces = jnp.split(shard, lax.axis_size(name), axis=split)
+    received = lax.all_to_all(jnp.stack(pieces), name, 0, 0)
+    return jnp.concatenate(received, axis=join)
 
 
 def doc_index(positions, doc_ends):
@@ -81,7 +87,7 @@
     )
     final_max, final_sum, final_out = lax.fori_loop(0, stretch_span + 1, one_tile, start_state)
     attended = (final_out / final_sum[..., None]).reshape(tok_rows, q_cols).astype(jnp.bfloat16)
-    return lax.all_to_all(attended, "tp", split_axis=0, concat_axis=1, tiled=True)
+    return stacked_exchange(attended, "tp", 0, 1)
 
 
 def solution(mesh):

time: 254 us -> 252 us (level)
    convert_element_type x2 -> x1, local copies, waits for them, and re-layouts: 7.04 us -> 2.03 us  [on_device(): (final_out / final_sum[..., None]).reshape(tok_rows, q_cols)]
    another operation x0 -> x2, local copies, waits for them, and re-layouts: none -> 3.02 us  [stacked_exchange(): received = lax.all_to_all(jnp.stack(pieces), name, 0, 0)]
    unnamed x2 -> x3, local copies, waits for them, and re-layouts: 9.53 us -> 9.92 us
where the time goes in v1:
time: 252 us; the launch traced here: 250 us
  blocking collectives  50.4 us (20%)
  local copies, waits for them, and re-layouts  43.7 us (17%)
  matrix products  42.8 us (17%)
  waiting for transfers between devices  39.5 us (16%)
  loops' own time  36.9 us (15%)
  other arithmetic  23.7 us (9%)
  between operations  13.5 us (5%)
    all_to_all x1, blocking collectives, stacked_exchange(): received = lax.all_to_all(jnp.stack(pieces), name, 0, 0)  50.4 us
    all_gather x1, waiting for transfers between devices, on_device(): kv_bank = lax.all_gather(paired[None], 'cp', axis=0, tiled=True)  39.5 us
    another operation x1, loops' own time, on_device(): lax.fori_loop(0, stretch_span + 1, one_tile, start_state)  36.9 us
    dot_general x5, matrix products, one_tile(): jnp.einsum('cqhjk,ckhd->cqhjd', weights.astype(jnp.bfloat16), pieces[:, 1...  32.5 us
    reduce_sum x5, other arithmetic, one_tile(): new_sum = rescale * running_sum + jnp.sum(weights, axis=-1)  14.3 us
    dot_general x5, matrix products, one_tile(): jnp.einsum('cqhjd,ckhd->cqhjk', q_blocks, pieces[:, 0], preferred_element...  10.2 us
    unnamed x3, local copies, waits for them, and re-layouts  9.92 us
    reshape x1, local copies, waits for them, and re-layouts, on_device(): kv_bank = kv_bank.reshape(bank_slots, 2, 2, half_rows, kv_local, HEAD)  9.75 us
  transfers between devices with their start and end apart: 1, of which 1 were waited for; matrix products, arithmetic and copies ran while one was open for 4% of the time, Pallas kernels for 0%

profile of v1, /device:TPU:0, one launch (start us, length us, event | category | flops | bytes accessed | tf_op | source)
XLA Modules:
  0.0 250.5 jit_solution(3112192983296691636)
XLA Ops:
  6.5 2.1 pad_maximum_fusion.2
  9.5 5.7 %reshape.171 = bf16[2,384,2,5,128]{4,3,2,1,0:T(8,128)(2,1)} reshape(bf16[768,1280]{1,0:T(8,128)(2,1)} %param.6) | data formatting | bytes 3932160 | tf_op jit(solution)/shard_map/reshape | solution.py:39
  15.2 2.4 copy.42
  17.9 39.5 %all-gather.3.cloned.1.call-done = bf16[16,768,256]{2,1,0:T(8,128)(2,1)} async-done(((bf16[2,768,256]{2,1,0:T(8,128)(2,1)}), bf16[16,768,256]{2,1,0:T(8,128)(2,1)}) %all-gather.3.cloned.1.call-update) | async-done | bytes 6291472 | tf_op jit(solution)/shard_map/all_gather | solution.py:32
  57.4 9.8 %reshape.163 = bf16[8,2,2,384,2,128]{5,4,3,2,1,0:T(2,128)(2,1)} reshape(bf16[16,768,256]{2,1,0:T(8,128)(2,1)} %all-gather.3.cloned.1.call-done) | data formatting | bytes 12582912 | tf_op jit(solution)/shard_map/reshape | solution.py:34
  67.1 7.1 %copy.41 = bf16[8,2,2,384,2,128]{5,3,4,1,2,0:T(8,128)(2,1)} copy(bf16[8,2,2,384,2,128]{5,4,3,2,1,0:T(2,128)(2,1)} %reshape.163) | data formatting | bytes 12582912
  74.2 108.8 %while.21 = (s32[]{:T(128)}, f32[2,384,2,5]{1,3,2,0:T(8,128)S(1)}, f32[2,384,2,5]{1,3,2,0:T(8,128)S(1)}, f32[2,384,2,5,128]{1,4,3,2,0:T(8,128)}, s32[2]{0:T(128)...) while((s32[]{:T(128)}, f32[2,384,2,5]{1,3,2,0:T(8,128)S(1)}, ...), condition=%wide.region_6.7_spmd.clone, body=%wide.region_2.6_spmd.clone.sunk | while | flops 1554047232 | bytes 50061820 | solution.py:88
  83.3 1.2 dynamic-slice_bitcast_fusion.3
  84.5 2.0 fusion.42
  86.5 2.9 %fusion.43 = f32[2,384,2,5]{1,3,2,0:T(8,128)S(1)} fusion(f32[2,2,384,384,5]{3,2,4,1,0:T(8,128)S(1)} %get-tuple-element.512, f32[2,384,2,5]{1,3,2,0:T(8,128)S(1)} %select_maximum_fusion.2, pred[2,384,384]{1,2,0:T(8,128)(4,1)S(1)} %compare_and_fusion.2), kind=kLoop, calls=%fused_computation.6.clone.1 | loop fusion | flops 14737920 | bytes 12152832 | tf_op jit(solution)/shard_map/while/body/eval_jaxpr/reduce_sum | solution.py:73
  89.4 5.3 %bitcast_add_fusion.2 = f32[2,384,2,5,128]{1,4,3,2,0:T(8,128)} fusion(f32[2,384,2,5,128]{1,4,3,2,0:T(8,128)} %get-tuple-element.533, f32[2,2,384,384,5]{3,2,4,1,0:T(8,128)S(1)} %get-tuple-element.512, f32[2,384,2,5]{1,3,2,0:T(8,128)S(1)} %select_maximum_fusion.2, pred[2,384,384]{1,2,0:T(8,128)(4,1)S(1)} %compare_and_fusion.2, ...), kind=kOutput, calls=%fused_computation.9.clone.1 | convolution fusion | flops 773455872 | bytes 20803584 | tf_op jit(solution)/shard_map/while/body/eval_jaxpr/cqhjk,ckhd->cqhjd/dot_general | solution.py:74
  103.8 1.2 dynamic-slice_bitcast_fusion.3
  105.0 2.0 fusion.42
  107.1 2.9 %fusion.43 = f32[2,384,2,5]{1,3,2,0:T(8,128)S(1)} fusion(f32[2,2,384,384,5]{3,2,4,1,0:T(8,128)S(1)} %get-tuple-element.512, f32[2,384,2,5]{1,3,2,0:T(8,128)S(1)} %select_maximum_fusion.2, pred[2,384,384]{1,2,0:T(8,128)(4,1)S(1)} %compare_and_fusion.2), kind=kLoop, calls=%fused_computation.6.clone.1 | loop fusion | flops 14737920 | bytes 12152832 | tf_op jit(solution)/shard_map/while/body/eval_jaxpr/reduce_sum | solution.py:73
  110.0 6.8 %bitcast_add_fusion.2 = f32[2,384,2,5,128]{1,4,3,2,0:T(8,128)} fusion(f32[2,384,2,5,128]{1,4,3,2,0:T(8,128)} %get-tuple-element.533, f32[2,2,384,384,5]{3,2,4,1,0:T(8,128)S(1)} %get-tuple-element.512, f32[2,384,2,5]{1,3,2,0:T(8,128)S(1)} %select_maximum_fusion.2, pred[2,384,384]{1,2,0:T(8,128)(4,1)S(1)} %compare_and_fusion.2, ...), kind=kOutput, calls=%fused_computation.9.clone.1 | convolution fusion | flops 773455872 | bytes 20803584 | tf_op jit(solution)/shard_map/while/body/eval_jaxpr/cqhjk,ckhd->cqhjd/dot_general | solution.py:74
  125.9 1.2 dynamic-slice_bitcast_fusion.3
  127.1 2.0 fusion.42
  129.1 2.9 %fusion.43 = f32[2,384,2,5]{1,3,2,0:T(8,128)S(1)} fusion(f32[2,2,384,384,5]{3,2,4,1,0:T(8,128)S(1)} %get-tuple-element.512, f32[2,384,2,5]{1,3,2,0:T(8,128)S(1)} %select_maximum_fusion.2, pred[2,384,384]{1,2,0:T(8,128)(4,1)S(1)} %compare_and_fusion.2), kind=kLoop, calls=%fused_computation.6.clone.1 | loop fusion | flops 14737920 | bytes 12152832 | tf_op jit(solution)/shard_map/while/body/eval_jaxpr/reduce_sum | solution.py:73
  132.1 6.8 %bitcast_add_fusion.2 = f32[2,384,2,5,128]{1,4,3,2,0:T(8,128)} fusion(f32[2,384,2,5,128]{1,4,3,2,0:T(8,128)} %get-tuple-element.533, f32[2,2,384,384,5]{3,2,4,1,0:T(8,128)S(1)} %get-tuple-element.512, f32[2,384,2,5]{1,3,2,0:T(8,128)S(1)} %select_maximum_fusion.2, pred[2,384,384]{1,2,0:T(8,128)(4,1)S(1)} %compare_and_fusion.2, ...), kind=kOutput, calls=%fused_computation.9.clone.1 | convolution fusion | flops 773455872 | bytes 20803584 | tf_op jit(solution)/shard_map/while/body/eval_jaxpr/cqhjk,ckhd->cqhjd/dot_general | solution.py:74
  148.0 1.2 dynamic-slice_bitcast_fusion.3
  149.1 2.0 fusion.42
  151.2 2.9 %fusion.43 = f32[2,384,2,5]{1,3,2,0:T(8,128)S(1)} fusion(f32[2,2,384,384,5]{3,2,4,1,0:T(8,128)S(1)} %get-tuple-element.512, f32[2,384,2,5]{1,3,2,0:T(8,128)S(1)} %select_maximum_fusion.2, pred[2,384,384]{1,2,0:T(8,128)(4,1)S(1)} %compare_and_fusion.2), kind=kLoop, calls=%fused_computation.6.clone.1 | loop fusion | flops 14737920 | bytes 12152832 | tf_op jit(solution)/shard_map/while/body/eval_jaxpr/reduce_sum | solution.py:73
  154.1 6.8 %bitcast_add_fusion.2 = f32[2,384,2,5,128]{1,4,3,2,0:T(8,128)} fusion(f32[2,384,2,5,128]{1,4,3,2,0:T(8,128)} %get-tuple-element.533, f32[2,2,384,384,5]{3,2,4,1,0:T(8,128)S(1)} %get-tuple-element.512, f32[2,384,2,5]{1,3,2,0:T(8,128)S(1)} %select_maximum_fusion.2, pred[2,384,384]{1,2,0:T(8,128)(4,1)S(1)} %compare_and_fusion.2, ...), kind=kOutput, calls=%fused_computation.9.clone.1 | convolution fusion | flops 773455872 | bytes 20803584 | tf_op jit(solution)/shard_map/while/body/eval_jaxpr/cqhjk,ckhd->cqhjd/dot_general | solution.py:74
  170.0 1.2 dynamic-slice_bitcast_fusion.3
  171.2 2.0 fusion.42
  173.3 2.9 %fusion.43 = f32[2,384,2,5]{1,3,2,0:T(8,128)S(1)} fusion(f32[2,2,384,384,5]{3,2,4,1,0:T(8,128)S(1)} %get-tuple-element.512, f32[2,384,2,5]{1,3,2,0:T(8,128)S(1)} %select_maximum_fusion.2, pred[2,384,384]{1,2,0:T(8,128)(4,1)S(1)} %compare_and_fusion.2), kind=kLoop, calls=%fused_computation.6.clone.1 | loop fusion | flops 14737920 | bytes 12152832 | tf_op jit(solution)/shard_map/while/body/eval_jaxpr/reduce_sum | solution.py:73
  176.2 6.8 %bitcast_add_fusion.2 = f32[2,384,2,5,128]{1,4,3,2,0:T(8,128)} fusion(f32[2,384,2,5,128]{1,4,3,2,0:T(8,128)} %get-tuple-element.533, f32[2,2,384,384,5]{3,2,4,1,0:T(8,128)S(1)} %get-tuple-element.512, f32[2,384,2,5]{1,3,2,0:T(8,128)S(1)} %select_maximum_fusion.2, pred[2,384,384]{1,2,0:T(8,128)(4,1)S(1)} %compare_and_fusion.2, ...), kind=kOutput, calls=%fused_computation.9.clone.1 | convolution fusion | flops 773455872 | bytes 20803584 | tf_op jit(solution)/shard_map/while/body/eval_jaxpr/cqhjk,ckhd->cqhjd/dot_general | solution.py:74
  183.0 2.5 %divide_convert_fusion = bf16[2,384,2,5,128]{1,4,3,2,0:T(8,128)(2,1)S(1)} fusion(f32[2,384,2,5,128]{1,4,3,2,0:T(8,128)} %get-tuple-element.300, f32[2,384,2,5]{1,3,2,0:T(8,128)S(1)} %get-tuple-element.301), kind=kLoop, calls=%fused_computation.40 | loop fusion | flops 1966080 | bytes 5928960 | tf_op jit(solution)/shard_map/convert_element_type | solution.py:89
  185.6 2.0 copy.43
  189.3 2.4 copy.46
  191.7 50.4 %all_to_all.5 = bf16[4,192,1280]{2,1,0:T(8,128)(2,1)S(1)} all-to-all(bf16[4,192,1280]{2,1,0:T(8,128)(2,1)} %copy.46), channel_id=1, replica_groups=mesh['cp'=8,'tp'=4] {'tp'}, dimensions={0} | all-to-all | bytes 3932160 | tf_op jit(solution)/shard_map/all_to_all | solution.py:13
  242.1 1.5 copy.56
  (62 shorter events, 11.7 us)
Async XLA Ops:
  6.5 50.8 %all-gather.3.cloned.1.call-start = ((), (), s32[]{:S(2)}) async-start(), calls=%async_computation.1 | async-start | bytes 7077888 | tf_op jit(solution)/shard_map/all_gather | solution.py:32
Sparse Core Ops, SparseCore 0:
  9.2 48.1 all-gather.2
